TPU v7x, 32 devices: a whole 2x2x4 slice. The times are simulated.
32 devices in a mesh: section: 4 (over y, x), dp: 8 (over z, core).
Axes of the slice: x: 2, y: 2, z: 4, core: 2. Of those that a mesh axis runs over, the one named last changes fastest.
Arguments:
- activations: bfloat16 [4, 8, 257, 1792], P('section', 'dp'), may hold values from -6 to 6
- saved: bfloat16 [4, 8, 257, 1792], P('section', 'dp'), may hold values from -6 to 6
- cotangents: bfloat16 [4, 8, 257, 1792], P('section', 'dp'), may hold values from -1.1953125 to 1.1953125
- projection: bfloat16 [4, 1792, 1792], P('section'), may hold values from -0.125 to 0.125
- section_gain: float32 [4, 1792], P('section'), may hold values from 0.5 to 1.5
- final_gain: float32 [1792], replicated, may hold values from 0.5 to 1.5
- head_weight: bfloat16 [1792, 1024], P('section'), may hold values from -0.125 to 0.125
- text_embed: bfloat16 [8, 1024], P('dp'), may hold values from -6 to 6
- labels: int32 [8], P('dp'), may hold values from 0 to 7, each once
Outputs:
- next_act: bfloat16 [4, 8, 257, 1792], P('section', 'dp')
- next_grad: bfloat16 [4, 8, 257, 1792], P('section', 'dp')
- mean_loss: float32 [4], P('section')
Inputs may be any that keep to these rules, and one draw needn't show every extreme that they name: labels holds each caption index once.
All inputs are finite; a program needn't handle non-finite values.
Results may differ from a plain program's by a relative error of at most 0.0039.
Values may be sent and summed in bfloat16 or wider, within the bound.
A program may use at most 64 MiB of HBM per device.

v0:
```python
import jax
import jax.numpy as jnp
from jax import lax
from jax.sharding import PartitionSpec as P

epsilon = 1e-06
logit_scale = 100.0


def shifted(value, axis, steps):
    count = lax.axis_size(axis)
    first, last = (max(0, -steps), min(count, count - steps))
    return lax.ppermute(value, axis, [(source, source + steps) for source in range(first, last)])


def spread(block, axis, owner):
    block = jnp.where(lax.axis_index(axis) == owner, block, jnp.zeros_like(block))
    return lax.psum(block, axis)


def norm_rows(values):
    centre = jnp.mean(values, axis=-1, keepdims=True)
    centred = values - centre
    variance = jnp.mean(centred * centred, axis=-1, keepdims=True)
    inverse = lax.rsqrt(variance + epsilon)
    return (centred * inverse, inverse)


def unit_rows(values):
    inverse = lax.rsqrt(jnp.sum(values * values, axis=-1, keepdims=True) + epsilon)
    return (values * inverse, inverse)


def forward_block(block_in, weight, scale_row):
    block_shape = block_in.shape
    standard, inverse = norm_rows(block_in.astype(jnp.float32))
    normed = (standard * scale_row).astype(jnp.bfloat16)
    mixed = jnp.dot(normed.reshape(-1, block_shape[-1]), weight, preferred_element_type=jnp.float32)
    return (block_in.astype(jnp.float32) + mixed.reshape(block_shape)).astype(jnp.bfloat16)


def backward_block(cotangent, restored, weight, scale_row):
    block_shape = restored.shape
    standard, inverse = norm_rows(restored.astype(jnp.float32))
    d_normed = lax.dot_general(
        cotangent.reshape(-1, block_shape[-1]),
        weight,
        (((1,), (1,)), ((), ())),
        preferred_element_type=jnp.float32,
    ).reshape(block_shape)
    d_standard = d_normed * scale_row
    d_input = cotangent.astype(jnp.float32) + inverse * (
        d_standard
        - jnp.mean(d_standard, axis=-1, keepdims=True)
        - standard * jnp.mean(d_standard * standard, axis=-1, keepdims=True)
    )
    return d_input.astype(jnp.bfloat16)


def contrastive(logits, label_values):
    count = logits.shape[0]
    targets = (label_values[:, None] == jnp.arange(count).astype(jnp.float32)[None, :]).astype(
        jnp.float32
    )
    row_lse = jax.nn.logsumexp(logits, axis=1)
    col_lse = jax.nn.logsumexp(logits, axis=0)
    picked = jnp.sum(logits * targets, axis=1)
    col_picked = jnp.sum(col_lse[None, :] * targets, axis=1)
    loss_value = 0.5 * jnp.mean(row_lse - picked) + 0.5 * jnp.mean(col_picked - picked)
    row_prob = jnp.exp(logits - row_lse[:, None])
    col_prob = jnp.exp(logits - col_lse[None, :])
    d_logits = 0.5 * (row_prob - targets + (col_prob - targets))
    return (loss_value, d_logits)


def local(
    activations,
    saved,
    cotangents,
    projection,
    section_gain,
    final_gain,
    head_weight,
    text_embed,
    labels,
):
    sections = lax.axis_size("section")
    section_index = lax.axis_index("section")
    is_last = section_index == sections - 1
    weight = projection[0]
    scale_row = section_gain[0]
    incoming = activations[0]
    block_out = forward_block(incoming, weight, scale_row)
    next_act = shifted(block_out[None], "section", 1)
    d_input = backward_block(cotangents[0], saved[0], weight, scale_row)
    passed_grad = shifted(d_input[None], "section", -1)
    pooled = jnp.mean(block_out.astype(jnp.float32), axis=1)
    pooled_std, pooled_inv = norm_rows(pooled)
    pooled_norm = (pooled_std * final_gain).astype(jnp.bfloat16)
    shared = spread(pooled_norm, "section", sections - 1)
    row_count = head_weight.shape[0]
    my_columns = lax.dynamic_slice_in_dim(shared, section_index * row_count, row_count, 1)
    embedding = lax.psum(
        jnp.dot(my_columns, head_weight, preferred_element_type=jnp.float32), "section"
    )
    image_unit, image_inv = unit_rows(embedding)
    own_count = image_unit.shape[0]
    text_unit, text_inv = unit_rows(text_embed.astype(jnp.float32))
    all_image, all_text, all_labels = (
        lax.all_gather(image_unit, "dp", axis=0, tiled=True),
        lax.all_gather(text_unit, "dp", axis=0, tiled=True),
        lax.all_gather(labels.astype(jnp.float32), "dp", axis=0, tiled=True),
    )
    logits = logit_scale * jnp.dot(all_image, all_text.T, precision=lax.Precision.HIGHEST)
    loss_value, d_logits = contrastive(logits, all_labels)
    own_rows = lax.dynamic_slice_in_dim(d_logits, lax.axis_index("dp") * own_count, own_count, 0)
    d_image = logit_scale * jnp.dot(own_rows, all_text, precision=lax.Precision.HIGHEST)
    d_embedding = (
        (d_image - image_unit * jnp.sum(d_image * image_unit, axis=-1, keepdims=True)) * image_inv
    ).astype(jnp.bfloat16)
    partial_value = lax.dot_general(
        d_embedding, head_weight, (((1,), (1,)), ((), ())), preferred_element_type=jnp.float32
    )
    d_pooled_norm = lax.all_gather(partial_value, "section", axis=1, tiled=True)
    d_std = d_pooled_norm * final_gain
    d_pooled = pooled_inv * (
        d_std
        - jnp.mean(d_std, axis=-1, keepdims=True)
        - pooled_std * jnp.mean(d_std * pooled_std, axis=-1, keepdims=True)
    )
    token_count = block_out.shape[1]
    loss_grad = jnp.broadcast_to((d_pooled / token_count)[:, None, :], block_out.shape).astype(
        jnp.bfloat16
    )
    next_grad = jnp.where(is_last, loss_grad[None], passed_grad)
    mean_loss = jnp.where(is_last, loss_value, jnp.float32(0.0))[None]
    return (next_act, next_grad, mean_loss)


def solution(mesh):
    return jax.shard_map(
        local,
        mesh=mesh,
        in_specs=(
            P("section", "dp", None, None),
            P("section", "dp", None, None),
            P("section", "dp", None, None),
            P("section", None, None),
            P("section", None),
            P(),
            P("section", None),
            P("dp", None),
            P("dp"),
        ),
        out_specs=(P("section", "dp", None, None), P("section", "dp", None, None), P("section")),
        check_vma=False,
    )
```

profile of v0, /device:TPU:0, one launch (start us, length us, event | category | flops | bytes accessed | tf_op | source)
XLA Modules:
  0.0 115.6 jit_solution(8883535703884968360)
XLA Ops:
  0.6 0.0 copy-start
  0.6 0.0 copy-start.2
  0.7 0.0 copy-start.6
  0.7 1.5 %convert_reduce_fusion = f32[257]{0:T(512)S(1)} fusion(bf16[1,1,257,1792]{3,2,1,0:T(8,128)(2,1)} %param.9), kind=kLoop, calls=%fused_computation.6 | loop fusion | flops 920831 | bytes 922116 | tf_op jit(solution)/shard_map/reduce_sum | solution.py:22
  2.2 1.6 %fusion.30 = f32[257]{0:T(512)S(1)} fusion(bf16[1,1,257,1792]{3,2,1,0:T(8,128)(2,1)} %param.9, f32[257]{0:T(512)S(1)} %broadcast_multiply_fusion.5), kind=kLoop, calls=%fused_computation.31 | loop fusion | flops 1841919 | bytes 923144 | tf_op jit(solution)/shard_map/reduce_sum | solution.py:24
  3.8 0.0 copy-done.6
  3.9 0.0 copy-done.2
  3.9 0.0 copy-start.1
  3.9 5.8 %convert_reduce_fusion.2 = (f32[1792]{0:T(1024)S(1)}, bf16[257,1792]{1,0:T(8,128)(2,1)}) fusion(bf16[1,1792,1792]{2,1,0:T(8,128)(2,1)} %param.12, bf16[1,1,257,1792]{3,2,1,0:T(8,128)(2,1)S(1)} %copy-done.2, f32[1792]{0:T(1024)S(1)} %reduce.23, f32[257]{0:T(512)S(1)} %add_rsqrt_fusion.1, f32[257]{0:T(512)S(1)} %broadcast_multiply_fusion.5), kind=kOutput, calls=%fused_computation.32 | convolution fusion | flops 1655193344 | bytes 8281096 | tf_op jit(solution)/shard_map/dot_general | solution.py:38
  9.7 5.0 %collective-permute-start = (bf16[1,1,257,1792]{3,2,1,0:T(8,128)(2,1)}, bf16[1,1,257,1792]{3,2,1,0:T(8,128)(2,1)S(1)}, u32[]{:S(2)}, u32[]{:S(2)}) collective-permute-start(bf16[1,1,257,1792]{3,2,1,0:T(8,128)(2,1)} %bitcast.4), channel_id=1, source_target_pairs={{0,8},{8,16},{16,24},{1,9},{9,17},{17,25},{2,10},{10,18},{18,26},{... | collective-permute-start | bytes 2763272 | tf_op jit(solution)/shard_map/ppermute | solution.py:13
  14.8 0.2 convert_reduce_fusion.1
  15.0 0.4 fusion.15
  15.4 4.9 %fusion.68 = (f32[257]{0:T(512)S(1)}, f32[257]{0:T(512)S(1)}, f32[257,1792]{1,0:T(8,128)S(1)}) fusion(f32[257]{0:T(512)S(1)} %add_rsqrt_fusion, f32[257]{0:T(512)S(1)} %broadcast_multiply_fusion.4, bf16[1,1,257,1792]{3,2,1,0:T(8,128)(2,1)S(1)} %copy-done.1, f32[1792]{0:T(1024)S(1)} %reduce.23, bf16[1,1792,1792]{2,1,0:T(8,128)(2,1)} %param.12, ...), kind=kOutput, calls=%fused_computation.102 | convolution fusion | flops 1653812992 | bytes 10118160 | tf_op jit(solution)/shard_map/dot_general | solution.py:45
  20.4 0.0 copy-start.5
  20.4 0.0 copy-start.8
  20.4 0.0 copy-start.4
  20.4 0.0 copy-start.7
  20.4 0.8 fusion.33
  21.2 1.3 %collective-permute-start.1 = (bf16[1,1,257,1792]{3,2,1,0:T(8,128)(2,1)S(1)}, bf16[1,1,257,1792]{3,2,1,0:T(8,128)(2,1)}, u32[]{:S(2)}, u32[]{:S(2)}) collective-permute-start(bf16[1,1,257,1792]{3,2,1,0:T(8,128)(2,1)S(1)} %fusion.33), channel_id=1, source_target_pairs={{8,0},{16,8},{24,16},{9,1},{17,9},{25,17},{10,2},{18,10},{26,18},{... | collective-permute-start | bytes 2763272 | tf_op jit(solution)/shard_map/ppermute | solution.py:13
  23.2 0.6 multiply_reduce_fusion.4
  24.5 0.6 dynamic-slice
  25.1 0.7 convert_dynamic-update-slice_fusion
  25.8 16.4 %all-reduce = f32[8]{0:T(128)S(1)} all-reduce(f32[8]{0:T(128)S(1)} %convert_dynamic-update-slice_fusion), channel_id=1, replica_groups=mesh['section'=4,'dp'=8] {'dp'}, use_global_device_ids=true, to_apply=%add | all-reduce | flops 8 | bytes 64
  42.2 14.1 %all-gather.2 = f32[8,1,1024]{2,1,0:T(1,128)S(1)} all-gather(f32[1,1,1024]{2,1,0:T(1,128)S(1)} %multiply_bitcast_fusion), channel_id=1, replica_groups=mesh['section'=4,'dp'=8] {'dp'}, dimensions={0}, use_global_device_ids=true | all-gather | bytes 36864 | tf_op jit(solution)/shard_map/all_gather | solution.py:111
  56.3 0.6 multiply_reduce_fusion.2
  57.5 0.6 multiply_reduce_fusion.1
  58.9 11.8 %psum.14 = bf16[1,1792]{1,0:T(2,128)(2,1)S(1)} all-reduce(bf16[1,1792]{1,0:T(2,128)(2,1)S(1)} %select_n.52), channel_id=1, replica_groups=mesh['section'=4,'dp'=8] {'section'}, use_global_device_ids=true, to_apply=%region_5.0 | all-reduce | flops 1792 | bytes 7168 | tf_op jit(solution)/shard_map/psum | solution.py:18
  70.7 0.3 fusion.58
  70.9 7.9 %psum.15 = f32[1,1024]{1,0:T(1,128)S(1)} all-reduce(f32[1,1024]{1,0:T(1,128)S(1)} %fusion.58), channel_id=1, replica_groups=mesh['section'=4,'dp'=8] {'section'}, use_global_device_ids=true, to_apply=%region_6.0 | all-reduce | flops 1024 | bytes 8192 | tf_op jit(solution)/shard_map/psum | solution.py:103
  78.8 0.6 multiply_reduce_fusion.5
  80.1 14.1 %all-gather.1 = f32[8,1,1024]{2,1,0:T(1,128)S(1)} all-gather(f32[1,1,1024]{2,1,0:T(1,128)S(1)} %fusion.67), channel_id=1, replica_groups=mesh['section'=4,'dp'=8] {'dp'}, dimensions={0}, use_global_device_ids=true | all-gather | bytes 36864 | tf_op jit(solution)/shard_map/all_gather | solution.py:110
  94.2 0.3 fusion.70
  94.5 0.2 fusion.49
  94.8 0.2 fusion.50
  94.9 0.6 subtract_reduce_fusion
  95.6 0.1 fusion.48
  95.6 0.2 fusion.38
  95.8 0.0 copy-done.7
  95.8 0.6 dynamic-slice.1
  98.4 0.6 multiply_reduce_fusion.3
  99.0 1.0 fusion.52
  100.0 0.2 dynamic-update-slice.1
  100.2 9.2 %all-reduce.1 = f32[1792]{0:T(1024)S(1)} all-reduce(f32[1792]{0:T(1024)S(1)} %dynamic-update-slice.1), channel_id=2, replica_groups=mesh['section'=4,'dp'=8] {'section'}, use_global_device_ids=true, to_apply=%add.1 | all-reduce | flops 1792 | bytes 14336
  109.4 0.7 fusion.69
  111.4 0.0 collective-permute-done
  111.4 0.0 collective-permute-done.1
  111.4 2.2 %broadcast_select_fusion = bf16[1,1,257,1792]{3,2,1,0:T(8,128)(2,1)} fusion(bf16[1,1,257,1792]{3,2,1,0:T(8,128)(2,1)} %collective-permute-done.1, pred[]{:T(512)S(6)} %eq.8, bf16[1792]{0:T(1024)(128)(2,1)S(1)} %multiply_convert_fusion), kind=kLoop, calls=%fused_computation.40 | loop fusion | flops 460544 | bytes 1845761 | tf_op jit(solution)/shard_map/jit(_where)/select_n | solution.py:135
  113.6 0.9 copy.34
  (24 shorter events, 0.1 us)
Async XLA Ops:
  0.6 70.0 %copy-start = (bf16[448,1024]{1,0:T(8,128)(2,1)S(1)}, bf16[448,1024]{1,0:T(8,128)(2,1)}, u32[]{:S(2)}) copy-start(bf16[448,1024]{1,0:T(8,128)(2,1)} %param.15) | copy-start | bytes 2752516
  0.6 3.2 %copy-start.2 = (bf16[1,1,257,1792]{3,2,1,0:T(8,128)(2,1)S(1)}, bf16[1,1,257,1792]{3,2,1,0:T(8,128)(2,1)}, u32[]{:S(2)}) copy-start(bf16[1,1,257,1792]{3,2,1,0:T(8,128)(2,1)} %param.9) | copy-start | bytes 2763268
  0.7 3.2 %copy-start.6 = (f32[1,1792]{1,0:T(1,128)S(1)}, f32[1,1792]{1,0:T(1,128)}, u32[]{:S(2)}) copy-start(f32[1,1792]{1,0:T(1,128)} %param.13) | copy-start | bytes 21508
  3.9 10.9 %copy-start.1 = (bf16[1,1,257,1792]{3,2,1,0:T(8,128)(2,1)S(1)}, bf16[1,1,257,1792]{3,2,1,0:T(8,128)(2,1)}, u32[]{:S(2)}) copy-start(bf16[1,1,257,1792]{3,2,1,0:T(8,128)(2,1)} %param.10) | copy-start | bytes 2763268
  9.7 5.7 %copy-start.3 = (bf16[1,1,257,1792]{3,2,1,0:T(8,128)(2,1)S(1)}, bf16[1,1,257,1792]{3,2,1,0:T(8,128)(2,1)}, u32[]{:S(2)}) copy-start(bf16[1,1,257,1792]{3,2,1,0:T(8,128)(2,1)} %param.11) | copy-start | bytes 2763268
  9.7 101.7 %collective-permute-start = (bf16[1,1,257,1792]{3,2,1,0:T(8,128)(2,1)}, bf16[1,1,257,1792]{3,2,1,0:T(8,128)(2,1)S(1)}, u32[]{:S(2)}, u32[]{:S(2)}) collective-permute-start(bf16[1,1,257,1792]{3,2,1,0:T(8,128)(2,1)} %bitcast.4), channel_id=1, source_target_pairs={{0,8},{8,16},{16,24},{1,9},{9,17},{17,25},{2,10},{10,18},{18,26},{... | collective-permute-start | bytes 2763272 | tf_op jit(solution)/shard_map/ppermute | solution.py:13
  20.4 2.8 %copy-start.5 = (bf16[1,1024]{1,0:T(2,128)(2,1)S(1)}, bf16[1,1024]{1,0:T(2,128)(2,1)}, u32[]{:S(2)}) copy-start(bf16[1,1024]{1,0:T(2,128)(2,1)} %param.16) | copy-start | bytes 6148
  20.4 4.0 %copy-start.8 = (u32[32]{0:T(128)S(1)}, u32[32]{0:T(128)}, u32[]{:S(2)}) copy-start(u32[32]{0:T(128)} %constant.76) | copy-start | bytes 388
  20.4 38.4 %copy-start.4 = (f32[1792]{0:T(1024)S(1)}, f32[1792]{0:T(1024)}, u32[]{:S(2)}) copy-start(f32[1792]{0:T(1024)} %param.14) | copy-start | bytes 21508
  20.4 75.4 %copy-start.7 = (u32[32]{0:T(128)S(1)}, u32[32]{0:T(128)}, u32[]{:S(2)}) copy-start(u32[32]{0:T(128)} %constant.81) | copy-start | bytes 388
  21.2 90.2 %collective-permute-start.1 = (bf16[1,1,257,1792]{3,2,1,0:T(8,128)(2,1)S(1)}, bf16[1,1,257,1792]{3,2,1,0:T(8,128)(2,1)}, u32[]{:S(2)}, u32[]{:S(2)}) collective-permute-start(bf16[1,1,257,1792]{3,2,1,0:T(8,128)(2,1)S(1)} %fusion.33), channel_id=1, source_target_pairs={{8,0},{16,8},{24,16},{9,1},{17,9},{25,17},{10,2},{18,10},{26,18},{... | collective-permute-start | bytes 2763272 | tf_op jit(solution)/shard_map/ppermute | solution.py:13
where the time goes:
time: 116 us
  blocking collectives  73.4 us (63%)
  matrix products  12.5 us (11%)
  other arithmetic  12.4 us (11%)
  between operations  8.64 us (7%)
  starting transfers between devices  6.34 us (5%)
  local copies, waits for them, and re-layouts  2.44 us (2%)
    unnamed x2, blocking collectives  25.5 us
    all_gather x1, blocking collectives, local(): lax.all_gather(image_unit, 'dp', axis=0, tiled=True)  14.1 us
    all_gather x1, blocking collectives, local(): lax.all_gather(text_unit, 'dp', axis=0, tiled=True)  14.1 us
    psum x1, blocking collectives, spread(): return lax.psum(block, axis)  11.8 us
    psum x1, blocking collectives, local(): lax.psum(jnp.dot(my_columns, head_weight, preferred_element_type=jnp.floa...  7.87 us
    ppermute x2, starting transfers between devices, shifted(): lax.ppermute(value, axis, [(source, source + steps) for source in range(f...  6.34 us
    dot_general x1, matrix products, forward_block(): jnp.dot(normed.reshape(-1, block_shape[-1]), weight, preferred_element_ty...  5.82 us
    dot_general x1, matrix products, backward_block(): lax.dot_general(cotangent.reshape(-1, block_shape[-1]), weight, (((1,), (...  4.94 us
  transfers between devices with their start and end apart: 2, of which 0 were waited for; matrix products, arithmetic and copies ran while one was open for 13% of the time, Pallas kernels for 0%

commit v1 on v0

v1 whole, which is shorter than its diff:
```python
import functools

import jax
import jax.numpy as jnp
from jax import lax
from jax.experimental import pallas as pl
from jax.experimental.pallas import tpu as pltpu
from jax.sharding import PartitionSpec as P

epsilon = 1e-06
logit_scale = 100.0


def shifted(value, axis, steps):
    count = lax.axis_size(axis)
    first, last = (max(0, -steps), min(count, count - steps))
    return lax.ppermute(value, axis, [(source, source + steps) for source in range(first, last)])


def norm_rows(values):
    centre = jnp.mean(values, axis=-1, keepdims=True)
    centred = values - centre
    variance = jnp.mean(centred * centred, axis=-1, keepdims=True)
    inverse = lax.rsqrt(variance + epsilon)
    return (centred * inverse, inverse)


def forward_block(block_in, weight, scale_row):
    block_shape = block_in.shape
    standard, inverse = norm_rows(block_in.astype(jnp.float32))
    normed = (standard * scale_row).astype(jnp.bfloat16)
    mixed = jnp.dot(normed.reshape(-1, block_shape[-1]), weight, preferred_element_type=jnp.float32)
    return (block_in.astype(jnp.float32) + mixed.reshape(block_shape)).astype(jnp.bfloat16)


def backward_block(cotangent, restored, weight, scale_row):
    block_shape = restored.shape
    standard, inverse = norm_rows(restored.astype(jnp.float32))
    d_normed = lax.dot_general(
        cotangent.reshape(-1, block_shape[-1]),
        weight,
        (((1,), (1,)), ((), ())),
        preferred_element_type=jnp.float32,
    ).reshape(block_shape)
    d_standard = d_normed * scale_row
    d_input = cotangent.astype(jnp.float32) + inverse * (
        d_standard
        - jnp.mean(d_standard, axis=-1, keepdims=True)
        - standard * jnp.mean(d_standard * standard, axis=-1, keepdims=True)
    )
    return d_input.astype(jnp.bfloat16)


MESH = pl.DeviceIdType.MESH


def exchange(slots, send, recv, axis, me, peers):
    def start(step, carry):
        peer = lax.rem(me + step, peers)
        pltpu.make_async_remote_copy(
            slots.at[me], slots.at[me], send.at[peer], recv.at[me], {axis: peer}, MESH
        ).start()
        return carry

    lax.fori_loop(1, peers, start, 0)


def arrived(slots, send, recv, axis, me, peers):
    def wait(step, carry):
        peer = lax.rem(me + step, peers)
        pltpu.make_async_remote_copy(
            slots.at[me], slots.at[peer], send.at[peer], recv.at[peer], {axis: peer}, MESH
        ).wait_recv()
        return carry

    lax.fori_loop(1, peers, wait, 0)


def sent(slots, send, recv, axis, me, peers):
    def wait(step, carry):
        peer = lax.rem(me + step, peers)
        pltpu.make_async_remote_copy(
            slots.at[me], slots.at[me], send.at[peer], recv.at[peer], {axis: peer}, MESH
        ).wait_send()
        return carry

    lax.fori_loop(1, peers, wait, 0)


def enter(sections, replicas):
    section, replica = lax.axis_index("section"), lax.axis_index("dp")
    barrier = pltpu.get_barrier_semaphore()

    def greet_section(step, carry):
        peer = lax.rem(section + step, sections)
        pl.semaphore_signal(barrier, inc=1, device_id={"section": peer}, device_id_type=MESH)
        return carry

    def greet_replica(step, carry):
        peer = lax.rem(replica + step, replicas)
        pl.semaphore_signal(barrier, inc=1, device_id={"dp": peer}, device_id_type=MESH)
        return carry

    lax.fori_loop(1, sections, greet_section, 0)
    lax.fori_loop(1, replicas, greet_replica, 0)
    pl.semaphore_wait(barrier, sections + replicas - 2)


def total_mean(pieces, width):
    return jnp.sum(jnp.sum(pieces, axis=2, keepdims=True), axis=0, keepdims=True) / width


def loss_chain(
    sections,
    replicas,
    tokens,
    pooled_ref,
    gain_ref,
    head_ref,
    text_ref,
    label_ref,
    grad_ref,
    loss_ref,
    feats,
    feat_in,
    parts,
    images,
    texts,
    back,
    feat_send,
    feat_recv,
    part_send,
    part_recv,
    image_send,
    image_recv,
    text_send,
    text_recv,
    back_send,
    back_recv,
):
    section, replica = lax.axis_index("section"), lax.axis_index("dp")
    last = sections - 1
    rows = pooled_ref.shape[2]
    width = sections * rows
    span = text_ref.shape[1]
    text = text_ref[...].astype(jnp.float32)
    text_inv = lax.rsqrt(jnp.sum(text * text, axis=-1, keepdims=True) + epsilon)
    texts[replica, :, 0:span] = text * text_inv
    texts[replica, :, span:] = label_ref[...]
    pooled = pooled_ref[...]
    centred = pooled - total_mean(pooled, width)
    pooled_inv = lax.rsqrt(total_mean(centred * centred, width) + epsilon)
    pooled_std = centred * pooled_inv
    feats[...] = (pooled_std * gain_ref[...]).astype(jnp.bfloat16).astype(jnp.float32)
    enter(sections, replicas)

    @pl.when(section == last)
    def _():
        for peer in range(last):
            pltpu.make_async_remote_copy(
                feats.at[peer], feat_in, feat_send.at[peer], feat_recv, {"section": peer}, MESH
            ).start()
        feat_in[...] = feats[last]

    exchange(texts, text_send, text_recv, "dp", replica, replicas)

    @pl.when(section != last)
    def _():
        pltpu.make_async_remote_copy(
            feats.at[0], feat_in, feat_send.at[0], feat_recv, {"section": last}, MESH
        ).wait_recv()

    parts[section] = jnp.dot(
        feat_in[...].astype(jnp.bfloat16), head_ref[...], preferred_element_type=jnp.float32
    )
    exchange(parts, part_send, part_recv, "section", section, sections)
    arrived(texts, text_send, text_recv, "dp", replica, replicas)
    arrived(parts, part_send, part_recv, "section", section, sections)
    embedding = jnp.sum(parts[...], axis=0)
    image_inv = lax.rsqrt(jnp.sum(embedding * embedding, axis=-1, keepdims=True) + epsilon)
    image_unit = embedding * image_inv
    images[replica] = image_unit
    exchange(images, image_send, image_recv, "dp", replica, replicas)
    all_text = texts[:, 0, 0:span]
    label_column = texts[:, 0, span : span + 1]
    column = lax.broadcasted_iota(jnp.int32, (replicas, replicas), 1)
    row = lax.broadcasted_iota(jnp.int32, (replicas, replicas), 0)
    targets = jnp.where(label_column == column.astype(jnp.float32), 1.0, 0.0)
    arrived(images, image_send, image_recv, "dp", replica, replicas)
    all_image = images[:, 0, :]
    logits = logit_scale * lax.dot_general(
        all_image,
        all_text,
        (((1,), (1,)), ((), ())),
        precision=lax.Precision.HIGHEST,
        preferred_element_type=jnp.float32,
    )
    row_max = jnp.max(logits, axis=1, keepdims=True)
    row_lse = row_max + jnp.log(jnp.sum(jnp.exp(logits - row_max), axis=1, keepdims=True))
    col_max = jnp.max(logits, axis=0, keepdims=True)
    col_lse = col_max + jnp.log(jnp.sum(jnp.exp(logits - col_max), axis=0, keepdims=True))
    d_logits = 0.5 * ((jnp.exp(logits - row_lse) - targets) + (jnp.exp(logits - col_lse) - targets))
    own = jnp.sum(jnp.where(row == replica, d_logits, 0.0), axis=0, keepdims=True)
    d_image = logit_scale * jnp.dot(
        own, all_text, precision=lax.Precision.HIGHEST, preferred_element_type=jnp.float32
    )
    along = jnp.sum(d_image * image_unit, axis=-1, keepdims=True)
    d_embedding = ((d_image - image_unit * along) * image_inv).astype(jnp.bfloat16)
    back[section] = lax.dot_general(
        d_embedding,
        head_ref[...],
        (((1,), (1,)), ((), ())),
        preferred_element_type=jnp.float32,
    )

    @pl.when(section != last)
    def _():
        pltpu.make_async_remote_copy(
            back.at[section], back.at[section], back_send, back_recv.at[section], {"section": last}, MESH
        ).start()

    picked = jnp.sum(logits * targets, axis=1, keepdims=True)
    col_picked = jnp.sum(col_lse * targets, axis=1, keepdims=True)
    loss = 0.5 * (row_lse - picked) + 0.5 * (col_picked - picked)
    loss_ref[...] = jnp.broadcast_to(jnp.sum(loss, axis=0, keepdims=True) / replicas, loss_ref.shape)

    @pl.when(section == last)
    def _():
        for peer in range(last):
            pltpu.make_async_remote_copy(
                back.at[peer], back.at[peer], back_send, back_recv.at[peer], {"section": peer}, MESH
            ).wait_recv()

    d_std = back[...] * gain_ref[...]
    d_pooled = pooled_inv * (
        d_std - total_mean(d_std, width) - pooled_std * total_mean(d_std * pooled_std, width)
    )
    grad_ref[...] = d_pooled / tokens
    sent(texts, text_send, text_recv, "dp", replica, replicas)
    sent(images, image_send, image_recv, "dp", replica, replicas)
    sent(parts, part_send, part_recv, "section", section, sections)

    @pl.when(section == last)
    def _():
        for peer in range(last):
            pltpu.make_async_remote_copy(
                feats.at[peer], feat_in, feat_send.at[peer], feat_recv, {"section": peer}, MESH
            ).wait_send()

    @pl.when(section != last)
    def _():
        pltpu.make_async_remote_copy(
            back.at[section], back.at[section], back_send, back_recv.at[section], {"section": last}, MESH
        ).wait_send()


def run_chain(pooled, gain, head_weight, text, labels, tokens):
    sections, replicas = lax.axis_size("section"), lax.axis_size("dp")
    rows, span = head_weight.shape
    label_row = jnp.broadcast_to(labels.astype(jnp.float32)[:, None], (1, 128))
    f32 = jnp.float32
    dma = pltpu.SemaphoreType.DMA
    vmem = pl.BlockSpec(memory_space=pltpu.VMEM)
    return pl.pallas_call(
        functools.partial(loss_chain, sections, replicas, tokens),
        out_shape=(
            jax.ShapeDtypeStruct((sections, 1, rows), f32),
            jax.ShapeDtypeStruct((1, 128), f32),
        ),
        in_specs=[vmem] * 5,
        out_specs=(vmem, vmem),
        scratch_shapes=[
            pltpu.VMEM((sections, 1, rows), f32),
            pltpu.VMEM((1, rows), f32),
            pltpu.VMEM((sections, 1, span), f32),
            pltpu.VMEM((replicas, 1, span), f32),
            pltpu.VMEM((replicas, 1, span + 128), f32),
            pltpu.VMEM((sections, 1, rows), f32),
            dma((sections,)),
            dma,
            dma((sections,)),
            dma((sections,)),
            dma((replicas,)),
            dma((replicas,)),
            dma((replicas,)),
            dma((replicas,)),
            dma,
            dma((sections,)),
        ],
        compiler_params=pltpu.CompilerParams(collective_id=0, has_side_effects=True),
        cost_estimate=pl.CostEstimate(flops=100000000, bytes_accessed=1000000, transcendentals=0),
        name="loss_chain",
    )(
        pooled.reshape(sections, 1, rows),
        gain.reshape(sections, 1, rows),
        head_weight,
        text,
        label_row,
    )


def local(
    activations,
    saved,
    cotangents,
    projection,
    section_gain,
    final_gain,
    head_weight,
    text_embed,
    labels,
):
    sections = lax.axis_size("section")
    is_last = lax.axis_index("section") == sections - 1
    weight = projection[0]
    scale_row = section_gain[0]
    block_out = forward_block(activations[0], weight, scale_row)
    next_act = shifted(block_out[None], "section", 1)
    d_input = backward_block(cotangents[0], saved[0], weight, scale_row)
    passed_grad = shifted(d_input[None], "section", -1)
    pooled = jnp.mean(block_out.astype(jnp.float32), axis=1)
    grad_row, loss_row = run_chain(
        pooled, final_gain, head_weight, text_embed, labels, block_out.shape[1]
    )
    loss_grad = jnp.broadcast_to(
        grad_row.reshape(1, 1, -1).astype(jnp.bfloat16), block_out.shape
    )
    next_grad = jnp.where(is_last, loss_grad[None], passed_grad)
    mean_loss = jnp.where(is_last, loss_row[0, 0], jnp.float32(0.0))[None]
    return (next_act, next_grad, mean_loss)


def solution(mesh):
    return jax.shard_map(
        local,
        mesh=mesh,
        in_specs=(
            P("section", "dp", None, None),
            P("section", "dp", None, None),
            P("section", "dp", None, None),
            P("section", None, None),
            P("section", None),
            P(),
            P("section", None),
            P("dp", None),
            P("dp"),
        ),
        out_specs=(P("section", "dp", None, None), P("section", "dp", None, None), P("section")),
        check_vma=False,
    )
```

time: 116 us -> 71 us (0.61)
  blocking collectives: 73.4 us -> 0 us
  Pallas kernels: 0 us -> 41.1 us
  other arithmetic: 12.4 us -> 6.27 us
  between operations: 8.64 us -> 3.2 us
  matrix products: 12.5 us -> 10.8 us
    pallas_call x0 -> x1, Pallas kernels: none -> 41.1 us  [run_chain(): pl.pallas_call(functools.partial(loss_chain, sections, replicas, tokens),...]
    all_gather x2 -> x0, blocking collectives: 28.2 us -> none  [the longest x1 14.1 us: local(): lax.all_gather(image_unit, 'dp', axis=0, tiled=True)]
    unnamed x2 -> x0, blocking collectives: 25.5 us -> none
    psum x2 -> x0, blocking collectives: 19.7 us -> none  [the longest x1 11.8 us: spread(): return lax.psum(block, axis)]
    reduce_sum x7 -> x0, other arithmetic: 3.52 us -> none  [the longest x2 1.22 us: unit_rows(): jnp.sum(values * values, axis=-1, keepdims=True) + epsilon]
    dot_general x4 -> x0, matrix products: 1.72 us -> none  [the longest x1 0.99 us: local(): lax.dot_general(d_embedding, head_weight, (((1,), (1,)), ((), ())), prefe...]
    unnamed x23 -> x11, local copies, waits for them, and re-layouts: 2.43 us -> 0.96 us
    select_n x1, other arithmetic: 2.2 us -> 1 us  [local(): next_grad = jnp.where(is_last, loss_grad[None], passed_grad)]
  transfers between devices with their start and end apart: 2 -> 2, of which waited for: 0 -> 0; matrix products, arithmetic and copies ran while one was open for 13% -> 13% of each run, Pallas kernels for 0% -> 58%
where the time goes in v1:
time: 71 us; the launch traced here: 70.7 us
  Pallas kernels  41.1 us (58%)
  matrix products  10.8 us (15%)
  starting transfers between devices  6.34 us (9%)
  other arithmetic  6.27 us (9%)
  between operations  3.2 us (5%)
  local copies, waits for them, and re-layouts  2.94 us (4%)
    pallas_call x1, Pallas kernels, run_chain(): pl.pallas_call(functools.partial(loss_chain, sections, replicas, tokens),...  41.1 us
    ppermute x2, starting transfers between devices, shifted(): lax.ppermute(value, axis, [(source, source + steps) for source in range(f...  6.34 us
    dot_general x1, matrix products, forward_block(): jnp.dot(normed.reshape(-1, block_shape[-1]), weight, preferred_element_ty...  5.81 us
    dot_general x1, matrix products, backward_block(): lax.dot_general(cotangent.reshape(-1, block_shape[-1]), weight, (((1,), (...  4.96 us
    reduce_sum x2, other arithmetic, norm_rows(): variance = jnp.mean(centred * centred, axis=-1, keepdims=True)  2.02 us
    reduce_sum x2, other arithmetic, norm_rows(): centre = jnp.mean(values, axis=-1, keepdims=True)  1.71 us
  transfers between devices with their start and end apart: 2, of which 0 were waited for; matrix products, arithmetic and copies ran while one was open for 13% of the time, Pallas kernels for 58%

profile of v1, /device:TPU:0, one launch (start us, length us, event | category | flops | bytes accessed | tf_op | source)
XLA Modules:
  0.0 70.7 jit_solution(12177965635875526318)
XLA Ops:
  0.6 0.0 copy-start.1
  0.6 0.0 copy-start.4
  0.7 1.5 %convert_reduce_fusion = f32[257]{0:T(512)S(1)} fusion(bf16[1,1,257,1792]{3,2,1,0:T(8,128)(2,1)} %param.9), kind=kLoop, calls=%fused_computation.6 | loop fusion | flops 920831 | bytes 922116 | tf_op jit(solution)/shard_map/reduce_sum | solution.py:21
  2.1 1.6 %fusion.30 = f32[257]{0:T(512)S(1)} fusion(bf16[1,1,257,1792]{3,2,1,0:T(8,128)(2,1)} %param.9, f32[257]{0:T(512)S(1)} %broadcast_multiply_fusion.4), kind=kLoop, calls=%fused_computation.31 | loop fusion | flops 1841919 | bytes 923144 | tf_op jit(solution)/shard_map/reduce_sum | solution.py:23
  3.8 0.0 copy-done.4
  3.8 0.0 copy-done.1
  3.8 0.0 copy-start
  3.8 5.8 %convert_reduce_fusion.2 = (f32[1792]{0:T(1024)S(1)}, bf16[257,1792]{1,0:T(8,128)(2,1)}) fusion(bf16[1,1792,1792]{2,1,0:T(8,128)(2,1)} %param.12, bf16[1,1,257,1792]{3,2,1,0:T(8,128)(2,1)S(1)} %copy-done.1, f32[1792]{0:T(1024)S(1)} %reduce.12, f32[257]{0:T(512)S(1)} %add_rsqrt_fusion.1, f32[257]{0:T(512)S(1)} %broadcast_multiply_fusion.4), kind=kOutput, calls=%fused_computation.32 | convolution fusion | flops 1655193344 | bytes 8281096 | tf_op jit(solution)/shard_map/dot_general | solution.py:32
  9.6 0.0 copy-start.2
  9.6 5.0 %collective-permute-start = (bf16[1,1,257,1792]{3,2,1,0:T(8,128)(2,1)}, bf16[1,1,257,1792]{3,2,1,0:T(8,128)(2,1)S(1)}, u32[]{:S(2)}, u32[]{:S(2)}) collective-permute-start(bf16[1,1,257,1792]{3,2,1,0:T(8,128)(2,1)} %bitcast.4), channel_id=1, source_target_pairs={{0,8},{8,16},{16,24},{1,9},{9,17},{17,25},{2,10},{10,18},{18,26},{... | collective-permute-start | bytes 2763272 | tf_op jit(solution)/shard_map/ppermute | solution.py:17
  14.7 0.0 copy-done
  14.7 0.2 convert_reduce_fusion.1
  14.9 0.4 fusion.15
  15.4 0.0 copy-done.2
  15.4 5.0 %fusion.38 = (f32[257]{0:T(512)S(1)}, f32[257]{0:T(512)S(1)}, f32[257,1792]{1,0:T(8,128)S(1)}) fusion(f32[257]{0:T(512)S(1)} %add_rsqrt_fusion, f32[257]{0:T(512)S(1)} %broadcast_multiply_fusion.3, bf16[1,1,257,1792]{3,2,1,0:T(8,128)(2,1)S(1)} %copy-done, f32[1792]{0:T(1024)S(1)} %reduce.12, bf16[1,1792,1792]{2,1,0:T(8,128)(2,1)} %param.12, ...), kind=kOutput, calls=%fused_computation.48 | convolution fusion | flops 1653812992 | bytes 10118160 | tf_op jit(solution)/shard_map/dot_general | solution.py:39
  20.3 0.0 copy-start.3
  20.4 0.8 %fusion.33 = bf16[1,1,257,1792]{3,2,1,0:T(8,128)(2,1)S(1)} fusion(bf16[1,1,257,1792]{3,2,1,0:T(8,128)(2,1)S(1)} %copy-done, f32[257,1792]{1,0:T(8,128)S(1)} %get-tuple-element.9, bf16[1,1,257,1792]{3,2,1,0:T(8,128)(2,1)S(1)} %copy-done.2, f32[257]{0:T(512)S(1)} %get-tuple-element.12, f32[257]{0:T(512)S(1)} %broadcast_multiply_fusion.3, ...), kind=kLoop, calls=%fused_computation.34 | loop fusion | flops 4605440 | bytes 4609552 | tf_op jit(solution)/shard_map/broadcast_in_dim | solution.py:320
  21.1 1.3 %collective-permute-start.1 = (bf16[1,1,257,1792]{3,2,1,0:T(8,128)(2,1)S(1)}, bf16[1,1,257,1792]{3,2,1,0:T(8,128)(2,1)S(1)}, u32[]{:S(2)}, u32[]{:S(2)}) collective-permute-start(bf16[1,1,257,1792]{3,2,1,0:T(8,128)(2,1)S(1)} %fusion.33), channel_id=1, source_target_pairs={{8,0},{16,8},{24,16},{9,1},{17,9},{25,17},{10,2},{18,10},{26,18},{... | collective-permute-start | bytes 2763272 | tf_op jit(solution)/shard_map/ppermute | solution.py:17
  22.4 0.7 div.30.pooled_ref
  23.1 0.0 copy-done.3
  23.1 0.7 reshape.263.gain_ref
  24.4 0.5 broadcast_in_dim.12.label_ref
  25.0 41.1 %loss_chain.1 = (f32[4,1,448]{2,1,0:T(1,128)}, f32[1,128]{1,0:T(1,128)}) custom-call(f32[4,1,448]{2,1,0:T(1,128)} %div.30.pooled_ref, f32[4,1,448]{2,1,0:T(1,128)} %reshape.263.gain_ref, bf16[448,1024]{1,0:T(8,128)(2,1)} %head_ref.1, bf16[1,1024]{1,0:T(2,128)(2,1)} %text_ref.1, f32[1,128]{1,0:T(1,128)} %broadcast_in_dim.12.label_ref), custom_call_target="tpu_custom_call" | custom-call | flops 100000000 | bytes 1000000 | tf_op jit(solution)/shard_map/loss_chain/pallas_call | solution.py:264
  66.1 0.7 %convert_reduce_fusion.3 = bf16[4,448]{1,0:T(4,128)(2,1)S(1)} fusion(f32[4,1,448]{2,1,0:T(1,128)} %get-tuple-element.5), kind=kLoop, calls=%fused_computation.40 | loop fusion | flops 1792 | bytes 10752 | tf_op jit(solution)/shard_map/convert_element_type | solution.py:326
  66.9 0.1 convert_element_type.101
  67.6 0.0 collective-permute-done
  67.6 0.0 collective-permute-done.1
  67.6 1.0 %broadcast_select_fusion = bf16[1,1,257,1792]{3,2,1,0:T(8,128)(2,1)} fusion(bf16[1,1,257,1792]{3,2,1,0:T(8,128)(2,1)S(1)} %collective-permute-done.1, pred[]{:T(512)S(6)} %eq.3, bf16[1792]{0:T(1024)(128)(2,1)S(1)} %convert_element_type.101), kind=kLoop, calls=%fused_computation.39 | loop fusion | flops 460544 | bytes 1845761 | tf_op jit(solution)/shard_map/jit(_where)/select_n | solution.py:328
  68.6 0.9 %copy.14 = bf16[1,1,257,1792]{3,2,1,0:T(8,128)(2,1)} copy(bf16[1,1,257,1792]{3,2,1,0:T(8,128)(2,1)S(1)} %collective-permute-done) | data formatting | bytes 1842176
  (7 shorter events, 0.1 us)
Async XLA Ops:
  0.6 3.2 %copy-start.1 = (bf16[1,1,257,1792]{3,2,1,0:T(8,128)(2,1)S(1)}, bf16[1,1,257,1792]{3,2,1,0:T(8,128)(2,1)}, u32[]{:S(2)}) copy-start(bf16[1,1,257,1792]{3,2,1,0:T(8,128)(2,1)} %param.9) | copy-start | bytes 2763268
  0.6 3.1 %copy-start.4 = (f32[1,1792]{1,0:T(1,128)S(1)}, f32[1,1792]{1,0:T(1,128)}, u32[]{:S(2)}) copy-start(f32[1,1792]{1,0:T(1,128)} %param.13) | copy-start | bytes 21508
  3.8 10.9 %copy-start = (bf16[1,1,257,1792]{3,2,1,0:T(8,128)(2,1)S(1)}, bf16[1,1,257,1792]{3,2,1,0:T(8,128)(2,1)}, u32[]{:S(2)}) copy-start(bf16[1,1,257,1792]{3,2,1,0:T(8,128)(2,1)} %param.10) | copy-start | bytes 2763268
  9.6 5.7 %copy-start.2 = (bf16[1,1,257,1792]{3,2,1,0:T(8,128)(2,1)S(1)}, bf16[1,1,257,1792]{3,2,1,0:T(8,128)(2,1)}, u32[]{:S(2)}) copy-start(bf16[1,1,257,1792]{3,2,1,0:T(8,128)(2,1)} %param.11) | copy-start | bytes 2763268
  9.6 57.9 %collective-permute-start = (bf16[1,1,257,1792]{3,2,1,0:T(8,128)(2,1)}, bf16[1,1,257,1792]{3,2,1,0:T(8,128)(2,1)S(1)}, u32[]{:S(2)}, u32[]{:S(2)}) collective-permute-start(bf16[1,1,257,1792]{3,2,1,0:T(8,128)(2,1)} %bitcast.4), channel_id=1, source_target_pairs={{0,8},{8,16},{16,24},{1,9},{9,17},{17,25},{2,10},{10,18},{18,26},{... | collective-permute-start | bytes 2763272 | tf_op jit(solution)/shard_map/ppermute | solution.py:17
  20.3 2.8 %copy-start.3 = (f32[1792]{0:T(1024)S(1)}, f32[1792]{0:T(1024)}, u32[]{:S(2)}) copy-start(f32[1792]{0:T(1024)} %param.14) | copy-start | bytes 21508
  21.1 46.5 %collective-permute-start.1 = (bf16[1,1,257,1792]{3,2,1,0:T(8,128)(2,1)S(1)}, bf16[1,1,257,1792]{3,2,1,0:T(8,128)(2,1)S(1)}, u32[]{:S(2)}, u32[]{:S(2)}) collective-permute-start(bf16[1,1,257,1792]{3,2,1,0:T(8,128)(2,1)S(1)} %fusion.33), channel_id=1, source_target_pairs={{8,0},{16,8},{24,16},{9,1},{17,9},{25,17},{10,2},{18,10},{26,18},{... | collective-permute-start | bytes 2763272 | tf_op jit(solution)/shard_map/ppermute | solution.py:17

commit v2 on v0

v2 whole, which is shorter than its diff:
```python
import functools
import math

import jax
import jax.numpy as jnp
from jax import lax
from jax.experimental import pallas as pl
from jax.experimental.pallas import tpu as pltpu
from jax.sharding import PartitionSpec as P

epsilon = 1e-06
logit_scale = 100.0
MESH = pl.DeviceIdType.MESH


def exchange(slots, send, recv, axis, me, peers):
    def start(step, carry):
        peer = lax.rem(me + step, peers)
        pltpu.make_async_remote_copy(
            slots.at[me], slots.at[me], send.at[peer], recv.at[me], {axis: peer}, MESH
        ).start()
        return carry

    lax.fori_loop(1, peers, start, 0)


def arrived(slots, send, recv, axis, me, peers):
    def wait(step, carry):
        peer = lax.rem(me + step, peers)
        pltpu.make_async_remote_copy(
            slots.at[me], slots.at[peer], send.at[peer], recv.at[peer], {axis: peer}, MESH
        ).wait_recv()
        return carry

    lax.fori_loop(1, peers, wait, 0)


def sent(slots, send, recv, axis, me, peers):
    def wait(step, carry):
        peer = lax.rem(me + step, peers)
        pltpu.make_async_remote_copy(
            slots.at[me], slots.at[me], send.at[peer], recv.at[peer], {axis: peer}, MESH
        ).wait_send()
        return carry

    lax.fori_loop(1, peers, wait, 0)


def enter(sections, replicas):
    section, replica = lax.axis_index("section"), lax.axis_index("dp")
    barrier = pltpu.get_barrier_semaphore()

    def greet_section(step, carry):
        peer = lax.rem(section + step, sections)
        pl.semaphore_signal(barrier, inc=1, device_id={"section": peer}, device_id_type=MESH)
        return carry

    def greet_replica(step, carry):
        peer = lax.rem(replica + step, replicas)
        pl.semaphore_signal(barrier, inc=1, device_id={"dp": peer}, device_id_type=MESH)
        return carry

    lax.fori_loop(1, sections, greet_section, 0)
    lax.fori_loop(1, replicas, greet_replica, 0)
    pl.semaphore_wait(barrier, sections + replicas - 2)


def row_stats(values):
    width = values.shape[-1]
    centre = jnp.sum(values, axis=-1, keepdims=True) / width
    centred = values - centre
    variance = jnp.sum(centred * centred, axis=-1, keepdims=True) / width
    return centre, lax.rsqrt(variance + epsilon)


def step_kernel(
    sections,
    replicas,
    group,
    chunk,
    act_ref,
    saved_ref,
    cot_ref,
    weight_ref,
    head_ref,
    scale_ref,
    gain_ref,
    text_ref,
    label_ref,
    next_ref,
    grad_ref,
    loss_ref,
    act,
    saved,
    cot,
    weight,
    normed,
    block,
    d_input,
    slope,
    pooled,
    heads,
    feats,
    columns,
    images,
    texts,
    d_rows,
    part_out,
    part_in,
    load_sem,
    weight_sem,
    head_send,
    head_recv,
    fwd_send,
    fwd_recv,
    bwd_send,
    bwd_recv,
    fill_sem,
    feat_send,
    feat_recv,
    col_send,
    col_recv,
    image_send,
    image_recv,
    text_send,
    text_recv,
    part_send,
    part_recv,
):
    section, replica = lax.axis_index("section"), lax.axis_index("dp")
    last = sections - 1
    tokens, width = act.shape
    rows, span = head_ref.shape
    shards = width // chunk
    slot = lax.rem(replica, group)
    first = replica - slot
    shard = span // group
    f32, bf16 = jnp.float32, jnp.bfloat16

    def cut(index):
        return pl.ds(pl.multiple_of(index * chunk, chunk), chunk)

    def weight_load(index):
        return pltpu.make_async_copy(
            weight_ref.at[:, cut(index)], weight.at[:, cut(index)], weight_sem.at[index]
        )

    load_act = pltpu.make_async_copy(act_ref, act, load_sem.at[0])
    load_saved = pltpu.make_async_copy(saved_ref, saved, load_sem.at[1])
    load_cot = pltpu.make_async_copy(cot_ref, cot, load_sem.at[2])
    load_act.start()
    for index in range(shards):
        weight_load(index).start()
    load_saved.start()
    load_cot.start()
    enter(sections, replicas)

    my_columns = pl.ds(pl.multiple_of(slot * shard, shard), shard)

    def head_rows(owner):
        return pl.ds(pl.multiple_of(owner * rows, rows), rows)

    def head_copy(owner):
        return pltpu.make_async_remote_copy(
            head_ref.at[:, my_columns],
            heads.at[head_rows(owner), :],
            head_send,
            head_recv.at[owner],
            {"section": last},
            MESH,
        )

    own_head = pltpu.make_async_copy(
        head_ref.at[:, my_columns], heads.at[head_rows(last), :], head_send
    )

    @pl.when(section < last)
    def _():
        head_copy(section).start()

    @pl.when(section == last)
    def _():
        own_head.start()
        text = text_ref[...].astype(f32)
        text_inv = lax.rsqrt(jnp.sum(text * text, axis=-1, keepdims=True) + epsilon)
        texts[replica, :, 0:span] = text * text_inv
        texts[replica, :, span:] = label_ref[...]
        exchange(texts, text_send, text_recv, "dp", replica, replicas)

    load_act.wait()
    values = act[...].astype(f32)
    centre, inverse = row_stats(values)
    normed[...] = ((values - centre) * inverse * scale_ref[...]).astype(bf16)

    def forward_copy(index):
        return pltpu.make_async_remote_copy(
            block.at[:, cut(index)],
            next_ref.at[:, cut(index)],
            fwd_send.at[index],
            fwd_recv.at[index],
            {"section": section + 1},
            MESH,
        )

    def backward_copy(index):
        return pltpu.make_async_remote_copy(
            d_input.at[:, cut(index)],
            grad_ref.at[:, cut(index)],
            bwd_send.at[index],
            bwd_recv.at[index],
            {"section": section - 1},
            MESH,
        )

    def forward_step(index, carry):
        weight_load(index).wait()
        mixed = jnp.dot(normed[...], weight[:, cut(index)], preferred_element_type=f32)
        piece = (act[:, cut(index)].astype(f32) + mixed).astype(bf16)
        block[:, cut(index)] = piece
        pooled[:, cut(index)] = jnp.sum(piece.astype(f32), axis=0, keepdims=True) / tokens

        @pl.when(section < last)
        def _():
            forward_copy(index).start()

        return carry

    lax.fori_loop(0, shards, forward_step, 0)
    load_saved.wait()
    load_cot.wait()

    @pl.when(section > 0)
    def _():
        centre, inverse = row_stats(saved[...].astype(f32))

        def gradient_step(index, carry):
            sum_slope, sum_product = carry
            d_normed = lax.dot_general(
                cot[...],
                weight[cut(index), :],
                (((1,), (1,)), ((), ())),
                preferred_element_type=f32,
            )
            piece = d_normed * scale_ref[:, cut(index)]
            standard = (saved[:, cut(index)].astype(f32) - centre) * inverse
            slope[:, cut(index)] = piece
            return (
                sum_slope + jnp.sum(piece, axis=-1, keepdims=True),
                sum_product + jnp.sum(piece * standard, axis=-1, keepdims=True),
            )

        zero = jnp.zeros((tokens, 1), f32)
        sum_slope, sum_product = lax.fori_loop(0, shards, gradient_step, (zero, zero))
        mean_slope, mean_product = sum_slope / width, sum_product / width

        def emit_step(index, carry):
            standard = (saved[:, cut(index)].astype(f32) - centre) * inverse
            d_input[:, cut(index)] = (
                cot[:, cut(index)].astype(f32)
                + inverse * (slope[:, cut(index)] - mean_slope - standard * mean_product)
            ).astype(bf16)
            backward_copy(index).start()
            return carry

        lax.fori_loop(0, shards, emit_step, 0)

    loss_ref[...] = jnp.zeros_like(loss_ref)

    fill_next = pltpu.make_async_copy(normed, next_ref, fill_sem)
    fill_grad = pltpu.make_async_copy(block, grad_ref, fill_sem)

    @pl.when(section == 0)
    def _():
        normed[...] = jnp.zeros_like(normed)
        fill_next.start()
        fill_next.wait()

    @pl.when(section == last)
    def _():
        mean_row = pooled[...]
        centre, pooled_inv = row_stats(mean_row)
        pooled_std = (mean_row - centre) * pooled_inv
        feats[slot] = (pooled_std * gain_ref[...]).astype(bf16).astype(f32)

        def in_group(make):
            def go(step, carry):
                peer = lax.rem(slot + step, group)
                make(peer)
                return carry

            lax.fori_loop(1, group, go, 0)

        def feat_copy(peer, source):
            return pltpu.make_async_remote_copy(
                feats.at[slot],
                feats.at[source],
                feat_send.at[peer],
                feat_recv.at[source],
                {"dp": first + peer},
                MESH,
            )

        def col_copy(peer, source):
            return pltpu.make_async_remote_copy(
                columns.at[slot],
                columns.at[source],
                col_send.at[peer],
                col_recv.at[source],
                {"dp": first + peer},
                MESH,
            )

        def part_copy(peer, source):
            return pltpu.make_async_remote_copy(
                part_out.at[peer],
                part_in.at[source],
                part_send.at[peer],
                part_recv.at[source],
                {"dp": first + peer},
                MESH,
            )

        in_group(lambda peer: feat_copy(peer, slot).start())
        own_head.wait()
        for owner in range(last):
            head_copy(owner).wait_recv()
        in_group(lambda peer: feat_copy(peer, peer).wait_recv())
        columns[slot] = jnp.dot(
            feats[:, 0, :].astype(bf16), heads[...], preferred_element_type=f32
        )
        in_group(lambda peer: col_copy(peer, slot).start())
        arrived(texts, text_send, text_recv, "dp", replica, replicas)
        all_text = texts[:, 0, 0:span]
        label_column = texts[:, 0, span : span + 1]
        column = lax.broadcasted_iota(jnp.int32, (replicas, replicas), 1)
        targets = jnp.where(label_column == column.astype(f32), 1.0, 0.0)
        in_group(lambda peer: col_copy(peer, peer).wait_recv())
        embedding = jnp.concatenate([columns[index] for index in range(group)], axis=1)
        image_inv = lax.rsqrt(jnp.sum(embedding * embedding, axis=-1, keepdims=True) + epsilon)
        image_unit = embedding * image_inv
        member = lax.broadcasted_iota(jnp.int32, (group, 1), 0)
        if replicas == group:
            all_image = image_unit
        else:
            images[replica] = jnp.sum(
                jnp.where(member == slot, image_unit, 0.0), axis=0, keepdims=True
            )
            exchange(images, image_send, image_recv, "dp", replica, replicas)
            arrived(images, image_send, image_recv, "dp", replica, replicas)
            all_image = images[:, 0, :]
        logits = logit_scale * lax.dot_general(
            all_image,
            all_text,
            (((1,), (1,)), ((), ())),
            precision=lax.Precision.HIGHEST,
            preferred_element_type=f32,
        )
        row_max = jnp.max(logits, axis=1, keepdims=True)
        row_lse = row_max + jnp.log(jnp.sum(jnp.exp(logits - row_max), axis=1, keepdims=True))
        col_max = jnp.max(logits, axis=0, keepdims=True)
        col_lse = col_max + jnp.log(jnp.sum(jnp.exp(logits - col_max), axis=0, keepdims=True))
        d_logits = 0.5 * (
            (jnp.exp(logits - row_lse) - targets) + (jnp.exp(logits - col_lse) - targets)
        )
        if replicas != group:
            pick_row = lax.broadcasted_iota(jnp.int32, (group, replicas), 0) + first
            pick_column = lax.broadcasted_iota(jnp.int32, (group, replicas), 1)
            d_logits = jnp.dot(
                jnp.where(pick_row == pick_column, 1.0, 0.0),
                d_logits,
                precision=lax.Precision.HIGHEST,
                preferred_element_type=f32,
            )
        d_image = logit_scale * jnp.dot(
            d_logits, all_text, precision=lax.Precision.HIGHEST, preferred_element_type=f32
        )
        along = jnp.sum(d_image * image_unit, axis=-1, keepdims=True)
        d_rows[...] = (d_image - image_unit * along) * image_inv
        partial = lax.dot_general(
            d_rows[:, my_columns].astype(bf16),
            heads[...],
            (((1,), (1,)), ((), ())),
            preferred_element_type=f32,
        )
        for index in range(group):
            part_out[index] = partial[index : index + 1, :]
        in_group(lambda peer: part_copy(peer, slot).start())
        part_in[slot] = jnp.sum(jnp.where(member == slot, partial, 0.0), axis=0, keepdims=True)
        picked = jnp.sum(logits * targets, axis=1, keepdims=True)
        col_picked = jnp.sum(col_lse * targets, axis=1, keepdims=True)
        loss = 0.5 * (row_lse - picked) + 0.5 * (col_picked - picked)
        loss_ref[...] = jnp.broadcast_to(
            jnp.sum(loss, axis=0, keepdims=True) / replicas, loss_ref.shape
        )
        in_group(lambda peer: part_copy(peer, peer).wait_recv())
        d_std = jnp.sum(part_in[...], axis=0) * gain_ref[...]
        d_pooled = pooled_inv * (
            d_std
            - jnp.sum(d_std, axis=-1, keepdims=True) / width
            - pooled_std * (jnp.sum(d_std * pooled_std, axis=-1, keepdims=True) / width)
        )
        block[...] = jnp.broadcast_to((d_pooled / tokens).astype(bf16), block.shape)
        fill_grad.start()
        fill_grad.wait()
        in_group(lambda peer: feat_copy(peer, peer).wait_send())
        in_group(lambda peer: col_copy(peer, peer).wait_send())
        in_group(lambda peer: part_copy(peer, peer).wait_send())
        sent(texts, text_send, text_recv, "dp", replica, replicas)
        if replicas != group:
            sent(images, image_send, image_recv, "dp", replica, replicas)

    @pl.when(section < last)
    def _():
        head_copy(section).wait_send()

    def drain(index, carry):
        @pl.when(section < last)
        def _():
            forward_copy(index).wait_send()
            backward_copy(index).wait_recv()

        @pl.when(section > 0)
        def _():
            forward_copy(index).wait_recv()
            backward_copy(index).wait_send()

        return carry

    lax.fori_loop(0, shards, drain, 0)


def local(
    activations,
    saved,
    cotangents,
    projection,
    section_gain,
    final_gain,
    head_weight,
    text_embed,
    labels,
):
    sections, replicas = lax.axis_size("section"), lax.axis_size("dp")
    tokens, width = activations.shape[2:]
    rows, span = head_weight.shape
    group = math.gcd(replicas, span // 128)
    shard = span // group
    chunk = 256 if width % 256 == 0 else 128
    shards = width // chunk
    label_row = jnp.broadcast_to(labels.astype(jnp.float32)[:, None], (1, 128))
    f32, bf16 = jnp.float32, jnp.bfloat16
    dma = pltpu.SemaphoreType.DMA
    vmem = pl.BlockSpec(memory_space=pltpu.VMEM)
    whole = pl.BlockSpec(memory_space=pl.ANY)
    next_act, next_grad, loss_row = pl.pallas_call(
        functools.partial(step_kernel, sections, replicas, group, chunk),
        out_shape=(
            jax.ShapeDtypeStruct((tokens, width), bf16),
            jax.ShapeDtypeStruct((tokens, width), bf16),
            jax.ShapeDtypeStruct((1, 128), f32),
        ),
        in_specs=[whole] * 5 + [vmem] * 4,
        out_specs=(whole, whole, vmem),
        scratch_shapes=[
            pltpu.VMEM((tokens, width), bf16),
            pltpu.VMEM((tokens, width), bf16),
            pltpu.VMEM((tokens, width), bf16),
            pltpu.VMEM((width, width), bf16),
            pltpu.VMEM((tokens, width), bf16),
            pltpu.VMEM((tokens, width), bf16),
            pltpu.VMEM((tokens, width), bf16),
            pltpu.VMEM((tokens, width), f32),
            pltpu.VMEM((1, width), f32),
            pltpu.VMEM((sections * rows, shard), bf16),
            pltpu.VMEM((group, 1, width), f32),
            pltpu.VMEM((group, group, shard), f32),
            pltpu.VMEM((replicas, 1, span), f32),
            pltpu.VMEM((replicas, 1, span + 128), f32),
            pltpu.VMEM((group, span), f32),
            pltpu.VMEM((group, 1, width), f32),
            pltpu.VMEM((group, 1, width), f32),
            dma((3,)),
            dma((shards,)),
            dma,
            dma((sections,)),
            dma((shards,)),
            dma((shards,)),
            dma((shards,)),
            dma((shards,)),
            dma,
            dma((group,)),
            dma((group,)),
            dma((group,)),
            dma((group,)),
            dma((replicas,)),
            dma((replicas,)),
            dma((replicas,)),
            dma((replicas,)),
            dma((group,)),
            dma((group,)),
        ],
        compiler_params=pltpu.CompilerParams(collective_id=0, has_side_effects=True),
        name="tower_step",
    )(
        activations[0, 0],
        saved[0, 0],
        cotangents[0, 0],
        projection[0],
        head_weight,
        section_gain,
        final_gain[None],
        text_embed,
        label_row,
    )
    return (next_act[None, None], next_grad[None, None], loss_row[0, :1])


def solution(mesh):
    return jax.shard_map(
        local,
        mesh=mesh,
        in_specs=(
            P("section", "dp", None, None),
            P("section", "dp", None, None),
            P("section", "dp", None, None),
            P("section", None, None),
            P("section", None),
            P(),
            P("section", None),
            P("dp", None),
            P("dp"),
        ),
        out_specs=(P("section", "dp", None, None), P("section", "dp", None, None), P("section")),
        check_vma=False,
    )
```

time: 116 us -> 61.2 us (0.53)
  blocking collectives: 73.4 us -> 0 us
  Pallas kernels: 0 us -> 51.5 us
  matrix products: 12.5 us -> 0 us
  other arithmetic: 12.4 us -> 0 us
  starting transfers between devices: 6.34 us -> 0 us
  between operations: 8.64 us -> 2.96 us
  local copies, waits for them, and re-layouts: 2.44 us -> 6.17 us
    pallas_call x0 -> x1, Pallas kernels: none -> 51.5 us  [local(): pl.pallas_call(functools.partial(step_kernel, sections, replicas, group,...]
    all_gather x2 -> x0, blocking collectives: 28.2 us -> none  [the longest x1 14.1 us: local(): lax.all_gather(image_unit, 'dp', axis=0, tiled=True)]
    unnamed x2 -> x0, blocking collectives: 25.5 us -> none
    psum x2 -> x0, blocking collectives: 19.7 us -> none  [the longest x1 11.8 us: spread(): return lax.psum(block, axis)]
    dot_general x6 -> x0, matrix products: 12.5 us -> none  [the longest x1 5.82 us: forward_block(): jnp.dot(normed.reshape(-1, block_shape[-1]), weight, preferred_element_ty...]
    reduce_sum x13 -> x0, other arithmetic: 8.5 us -> none  [the longest x3 2.63 us: norm_rows(): variance = jnp.mean(centred * centred, axis=-1, keepdims=True)]
    ppermute x2 -> x0, starting transfers between devices: 6.34 us -> none  [shifted(): lax.ppermute(value, axis, [(source, source + steps) for source in range(f...]
    select_n x3 -> x0, other arithmetic: 2.21 us -> none  [the longest x1 2.2 us: local(): next_grad = jnp.where(is_last, loss_grad[None], passed_grad)]
  transfers between devices with their start and end apart: 2 -> 0, of which waited for: 0 -> 0; matrix products, arithmetic and copies ran while one was open for 13% -> 0% of each run, Pallas kernels for 0% -> 0%
where the time goes in v2:
time: 61.2 us; the launch traced here: 60.7 us
  Pallas kernels  51.5 us (84%)
  local copies, waits for them, and re-layouts  6.17 us (10%)
  between operations  2.96 us (5%)
    pallas_call x1, Pallas kernels, local(): pl.pallas_call(functools.partial(step_kernel, sections, replicas, group,...  51.5 us
    unnamed x2, local copies, waits for them, and re-layouts  4.36 us
    broadcast_in_dim x1, local copies, waits for them, and re-layouts, local(): final_gain[None]  1.29 us

profile of v2, /device:TPU:0, one launch (start us, length us, event | category | flops | bytes accessed | tf_op | source)
XLA Modules:
  0.0 60.7 jit_solution(12965022322082574954)
XLA Ops:
  1.3 0.5 broadcast_in_dim.19.label_ref
  1.8 1.3 %broadcast_in_dim.17.gain_ref = f32[1,1792]{1,0:T(1,128)} reshape(f32[1792]{0:T(1024)} %param.14) | data formatting | bytes 14336 | tf_op jit(solution)/shard_map/broadcast_in_dim | solution.py:511
  3.1 51.5 %tower_step.1 = (bf16[257,1792]{1,0:T(8,128)(2,1)}, bf16[257,1792]{1,0:T(8,128)(2,1)}, f32[1,128]{1,0:T(1,128)}) custom-call(bf16[257,1792]{1,0:T(8,128)(2,1)} %bitcast.12, bf16[257,1792]{1,0:T(8,128)(2,1)} %bitcast.13, bf16[257,1792]{1,0:T(8,128)(2,1)} %bitcast.14, bf16[1792,1792]{1,0:T(8,128)(2,1)} %bitcast.9, bf16[448,1024]{1,0:T(8,128)(2,1)} %head_ref.1, ...), custom_call_target="tpu_custom_call" | custom-call | tf_op jit(solution)/shard_map/tower_step/pallas_call | solution.py:455
  54.6 2.2 %copy.16 = bf16[1,1,257,1792]{3,2,1,0:T(8,128)(2,1)} copy(bf16[1,1,257,1792]{3,2,1,0:T(8,128)(2,1)} %bitcast.11) | data formatting | bytes 1842176
  56.8 2.2 %copy.17 = bf16[1,1,257,1792]{3,2,1,0:T(8,128)(2,1)} copy(bf16[1,1,257,1792]{3,2,1,0:T(8,128)(2,1)} %bitcast.10) | data formatting | bytes 1842176

commit v3 on v2

--- a/solution.py
+++ b/solution.py
@@ -89,6 +89,7 @@
     label_ref,
     next_ref,
     grad_ref,
+    row_ref,
     loss_ref,
     act,
     saved,
@@ -107,6 +108,7 @@
     d_rows,
     part_out,
     part_in,
+    relay,
     load_sem,
     weight_sem,
     head_send,
@@ -115,7 +117,6 @@
     fwd_recv,
     bwd_send,
     bwd_recv,
-    fill_sem,
     feat_send,
     feat_recv,
     col_send,
@@ -126,6 +127,8 @@
     text_recv,
     part_send,
     part_recv,
+    relay_recv,
+    pass_send,
 ):
     section, replica = lax.axis_index("section"), lax.axis_index("dp")
     last = sections - 1
@@ -184,36 +187,78 @@
         text = text_ref[...].astype(f32)
         text_inv = lax.rsqrt(jnp.sum(text * text, axis=-1, keepdims=True) + epsilon)
         texts[replica, :, 0:span] = text * text_inv
-        texts[replica, :, span:] = label_ref[...]
+        texts[replica, :, span:] = jnp.full((1, 128), label_ref[0]).astype(f32)
         exchange(texts, text_send, text_recv, "dp", replica, replicas)
 
-    load_act.wait()
-    values = act[...].astype(f32)
-    centre, inverse = row_stats(values)
-    normed[...] = ((values - centre) * inverse * scale_ref[...]).astype(bf16)
-
-    def forward_copy(index):
+    cutoff = tokens // 2 // 16 * 16
+    halves = (pl.ds(0, cutoff), pl.ds(cutoff, tokens - cutoff))
+
+    def move(source, target, send, recv, peer, half, index):
+        part = (halves[half], cut(index))
         return pltpu.make_async_remote_copy(
-            block.at[:, cut(index)],
-            next_ref.at[:, cut(index)],
-            fwd_send.at[index],
-            fwd_recv.at[index],
-            {"section": section + 1},
+            source.at[part],
+            target.at[part],
+            send.at[half, index],
+            recv.at[half, index],
+            {"section": peer},
             MESH,
         )
 
-    def backward_copy(index):
-        return pltpu.make_async_remote_copy(
-            d_input.at[:, cut(index)],
-            grad_ref.at[:, cut(index)],
-            bwd_send.at[index],
-            bwd_recv.at[index],
-            {"section": section - 1},
-            MESH,
-        )
+    def forward_copy(half, index):
+        return move(block, next_ref, fwd_send, fwd_recv, section + 1, half, index)
+
+    def backward_copy(half, index):
+        return move(d_input, grad_ref, bwd_send, bwd_recv, section - 1, half, index)
+
+    middle = sections // 2
+    relays = sections >= 4
+    forward_relay, backward_relay = middle + 1, middle - 2
+
+    def forward_detour(index):
+        return move(block, relay, fwd_send, relay_recv, forward_relay, 1, index)
+
+    def backward_detour(index):
+        return move(d_input, relay, bwd_send, relay_recv, backward_relay, 1, index)
+
+    def forward_pass(index):
+        return move(relay, next_ref, pass_send, fwd_recv, middle, 1, index)
+
+    def backward_pass(index):
+        return move(relay, grad_ref, pass_send, bwd_recv, middle - 1, 1, index)
+
+    def send_piece(direct, detour, origin, index):
+        direct(0, index).start()
+        if not relays:
+            direct(1, index).start()
+            return
+
+        @pl.when(section == origin)
+        def _():
+            detour(index).start()
+
+        @pl.when(section != origin)
+        def _():
+            direct(1, index).start()
+
+    def send_forward(index):
+        send_piece(forward_copy, forward_detour, middle - 1, index)
+
+    def send_backward(index):
+        send_piece(backward_copy, backward_detour, middle, index)
+
+    def relay_all(detour, onward):
+        def go(index, carry):
+            detour(index).wait_recv()
+            onward(index).start()
+            return carry
+
+        lax.fori_loop(0, shards, go, 0)
 
     def forward_step(index, carry):
-        weight_load(index).wait()
+        @pl.when(section < last)
+        def _():
+            weight_load(index).wait()
+
         mixed = jnp.dot(normed[...], weight[:, cut(index)], preferred_element_type=f32)
         piece = (act[:, cut(index)].astype(f32) + mixed).astype(bf16)
         block[:, cut(index)] = piece
@@ -221,16 +266,20 @@
 
         @pl.when(section < last)
         def _():
-            forward_copy(index).start()
+            send_forward(index)
 
         return carry
 
-    lax.fori_loop(0, shards, forward_step, 0)
-    load_saved.wait()
-    load_cot.wait()
-
-    @pl.when(section > 0)
-    def _():
+    def forward():
+        load_act.wait()
+        values = act[...].astype(f32)
+        centre, inverse = row_stats(values)
+        normed[...] = ((values - centre) * inverse * scale_ref[...]).astype(bf16)
+        lax.fori_loop(0, shards, forward_step, 0)
+
+    def backward():
+        load_saved.wait()
+        load_cot.wait()
         centre, inverse = row_stats(saved[...].astype(f32))
 
         def gradient_step(index, carry):
@@ -259,28 +308,47 @@
                 cot[:, cut(index)].astype(f32)
                 + inverse * (slope[:, cut(index)] - mean_slope - standard * mean_product)
             ).astype(bf16)
-            backward_copy(index).start()
+            send_backward(index)
             return carry
 
         lax.fori_loop(0, shards, emit_step, 0)
 
-    loss_ref[...] = jnp.zeros_like(loss_ref)
-
-    fill_next = pltpu.make_async_copy(normed, next_ref, fill_sem)
-    fill_grad = pltpu.make_async_copy(block, grad_ref, fill_sem)
+    @pl.when(section == last)
+    def _():
+        for index in range(shards):
+            weight_load(index).wait()
+        backward()
+
+    forward()
+
+    @pl.when((section > 0) & (section < last))
+    def _():
+        backward()
 
     @pl.when(section == 0)
     def _():
-        normed[...] = jnp.zeros_like(normed)
-        fill_next.start()
-        fill_next.wait()
+        load_saved.wait()
+        load_cot.wait()
+
+    loss_ref[...] = jnp.zeros_like(loss_ref)
+    row_ref[...] = jnp.zeros_like(row_ref)
+
+    if relays:
+
+        @pl.when(section == forward_relay)
+        def _():
+            relay_all(forward_detour, forward_pass)
+
+        @pl.when(section == backward_relay)
+        def _():
+            relay_all(backward_detour, backward_pass)
 
     @pl.when(section == last)
     def _():
         mean_row = pooled[...]
         centre, pooled_inv = row_stats(mean_row)
         pooled_std = (mean_row - centre) * pooled_inv
-        feats[slot] = (pooled_std * gain_ref[...]).astype(bf16).astype(f32)
+        feats[slot] = (pooled_std * gain_ref[...].reshape(1, width)).astype(bf16).astype(f32)
 
         def in_group(make):
             def go(step, carry):
@@ -393,15 +461,13 @@
             jnp.sum(loss, axis=0, keepdims=True) / replicas, loss_ref.shape
         )
         in_group(lambda peer: part_copy(peer, peer).wait_recv())
-        d_std = jnp.sum(part_in[...], axis=0) * gain_ref[...]
+        d_std = jnp.sum(part_in[...], axis=0) * gain_ref[...].reshape(1, width)
         d_pooled = pooled_inv * (
             d_std
             - jnp.sum(d_std, axis=-1, keepdims=True) / width
             - pooled_std * (jnp.sum(d_std * pooled_std, axis=-1, keepdims=True) / width)
         )
-        block[...] = jnp.broadcast_to((d_pooled / tokens).astype(bf16), block.shape)
-        fill_grad.start()
-        fill_grad.wait()
+        row_ref[...] = d_pooled / tokens
         in_group(lambda peer: feat_copy(peer, peer).wait_send())
         in_group(lambda peer: col_copy(peer, peer).wait_send())
         in_group(lambda peer: part_copy(peer, peer).wait_send())
@@ -414,15 +480,23 @@
         head_copy(section).wait_send()
 
     def drain(index, carry):
-        @pl.when(section < last)
-        def _():
-            forward_copy(index).wait_send()
-            backward_copy(index).wait_recv()
-
-        @pl.when(section > 0)
-        def _():
-            forward_copy(index).wait_recv()
-            backward_copy(index).wait_send()
+        for half in range(2):
+
+            @pl.when(section < last)
+            def _():
+                forward_copy(half, index).wait_send()
+                backward_copy(half, index).wait_recv()
+
+            @pl.when(section > 0)
+            def _():
+                forward_copy(half, index).wait_recv()
+                backward_copy(half, index).wait_send()
+
+        if relays:
+
+            @pl.when((section == forward_relay) | (section == backward_relay))
+            def _():
+                forward_pass(index).wait_send()
 
         return carry
 
@@ -447,20 +521,20 @@
     shard = span // group
     chunk = 256 if width % 256 == 0 else 128
     shards = width // chunk
-    label_row = jnp.broadcast_to(labels.astype(jnp.float32)[:, None], (1, 128))
     f32, bf16 = jnp.float32, jnp.bfloat16
     dma = pltpu.SemaphoreType.DMA
     vmem = pl.BlockSpec(memory_space=pltpu.VMEM)
     whole = pl.BlockSpec(memory_space=pl.ANY)
-    next_act, next_grad, loss_row = pl.pallas_call(
+    next_raw, grad_raw, grad_row, loss_row = pl.pallas_call(
         functools.partial(step_kernel, sections, replicas, group, chunk),
         out_shape=(
             jax.ShapeDtypeStruct((tokens, width), bf16),
             jax.ShapeDtypeStruct((tokens, width), bf16),
+            jax.ShapeDtypeStruct((1, width), f32),
             jax.ShapeDtypeStruct((1, 128), f32),
         ),
-        in_specs=[whole] * 5 + [vmem] * 4,
-        out_specs=(whole, whole, vmem),
+        in_specs=[whole] * 5 + [vmem] * 3 + [pl.BlockSpec(memory_space=pltpu.SMEM)],
+        out_specs=(whole, whole, vmem, vmem),
         scratch_shapes=[
             pltpu.VMEM((tokens, width), bf16),
             pltpu.VMEM((tokens, width), bf16),
@@ -479,15 +553,15 @@
             pltpu.VMEM((group, span), f32),
             pltpu.VMEM((group, 1, width), f32),
             pltpu.VMEM((group, 1, width), f32),
+            pltpu.VMEM((tokens, width), bf16),
             dma((3,)),
             dma((shards,)),
             dma,
             dma((sections,)),
-            dma((shards,)),
-            dma((shards,)),
-            dma((shards,)),
-            dma((shards,)),
-            dma,
+            dma((2, shards)),
+            dma((2, shards)),
+            dma((2, shards)),
+            dma((2, shards)),
             dma((group,)),
             dma((group,)),
             dma((group,)),
@@ -498,6 +572,8 @@
             dma((replicas,)),
             dma((group,)),
             dma((group,)),
+            dma((2, shards)),
+            dma((2, shards)),
         ],
         compiler_params=pltpu.CompilerParams(collective_id=0, has_side_effects=True),
         name="tower_step",
@@ -508,10 +584,13 @@
         projection[0],
         head_weight,
         section_gain,
-        final_gain[None],
+        final_gain,
         text_embed,
-        label_row,
+        labels,
     )
+    section = lax.axis_index("section")
+    next_act = jnp.where(section == 0, jnp.zeros_like(next_raw), next_raw)
+    next_grad = jnp.where(section == sections - 1, grad_row.astype(bf16), grad_raw)
     return (next_act[None, None], next_grad[None, None], loss_row[0, :1])
 
 

time: 61.2 us -> 51.5 us (0.84)
  the two profiles are of different devices: /device:TPU:0 before, /device:TPU:4 now
where the time goes in v3:
time: 51.5 us; the launch traced here: 51.2 us
  Pallas kernels  44.7 us (87%)
  other arithmetic  3.58 us (7%)
  between operations  2.97 us (6%)
    pallas_call x1, Pallas kernels, local(): pl.pallas_call(functools.partial(step_kernel, sections, replicas, group,...  44.7 us
    broadcast_in_dim x1, other arithmetic, local(): return (next_act[None, None], next_grad[None, None], loss_row[0, :1])  2.86 us

profile of v3, /device:TPU:4, one launch (start us, length us, event | category | flops | bytes accessed | tf_op | source)
XLA Modules:
  0.0 51.2 jit_solution(4552040773150889118)
XLA Ops:
  1.3 44.7 %tower_step.1 = (bf16[257,1792]{1,0:T(8,128)(2,1)}, bf16[257,1792]{1,0:T(8,128)(2,1)}, f32[1,1792]{1,0:T(1,128)}, f32[1,128]{1,0:T(1,128)}) custom-call(bf16[257,1792]{1,0:T(8,128)(2,1)} %bitcast.11, bf16[257,1792]{1,0:T(8,128)(2,1)} %bitcast.12, bf16[257,1792]{1,0:T(8,128)(2,1)} %bitcast.13, bf16[1792,1792]{1,0:T(8,128)(2,1)} %bitcast.10, ...), custom_call_target="tpu_custom_call" | custom-call | tf_op jit(solution)/shard_map/tower_step/pallas_call | solution.py:528
  46.0 0.7 %convert_reduce_fusion = bf16[1792]{0:T(1024)(128)(2,1)S(1)} fusion(f32[1,1792]{1,0:T(1,128)} %get-tuple-element.8), kind=kLoop, calls=%fused_computation.2 | loop fusion | flops 1792 | bytes 10752 | tf_op jit(solution)/shard_map/convert_element_type | solution.py:593
  46.7 2.9 %select_bitcast_fusion = (bf16[1,1,257,1792]{3,2,1,0:T(8,128)(2,1)}, bf16[1,1,257,1792]{3,2,1,0:T(8,128)(2,1)}) fusion(bf16[257,1792]{1,0:T(8,128)(2,1)} %get-tuple-element.9, pred[]{:T(512)S(6)} %eq.7, bf16[1792]{0:T(1024)(128)(2,1)S(1)} %convert_reduce_fusion, bf16[257,1792]{1,0:T(8,128)(2,1)} %get-tuple-element.7, pred[]{:T(512)S(6)} %eq.6), kind=kLoop, calls=%fused_computation | loop fusion | flops 921088 | bytes 3687938 | tf_op jit(solution)/shard_map/broadcast_in_dim | solution.py:594
